TPU v7x, 32 devices: a whole 2x2x4 slice. The times are simulated.
32 devices in a mesh: pipe: 4 (over z), expert: 4 (over y, x), tensor: 2 (over core).
Axes of the slice: x: 2, y: 2, z: 4, core: 2. Of those that a mesh axis runs over, the one named last changes fastest.
Arguments:
- inputs_prev: bfloat16 [4, 512, 3584], P('pipe', 'expert', 'tensor'), may hold values from -6 to 6
- cotangent_next: bfloat16 [4, 512, 3584], P('pipe', 'expert', 'tensor'), may hold values from -6 to 6
- saved_input: bfloat16 [4, 512, 3584], P('pipe', 'expert', 'tensor'), may hold values from -6 to 6
- expert_ids: int32 [2, 4, 512, 8], P(None, 'pipe', 'expert'), may hold values from 0 to 255, as said below
- keep_mask: int32 [2, 4, 512, 8], P(None, 'pipe', 'expert'), may hold values from 0 to 1, as said below
- slot_pos: int32 [2, 4, 512, 8], P(None, 'pipe', 'expert'), may hold values from 0 to 3, as said below
- weight_q: int32 [2, 4, 512, 8], P(None, 'pipe', 'expert'), may hold values from 1 to 4095
- gate_routed: bfloat16 [4, 4, 3584, 512], P('pipe', 'expert', None, 'tensor'), may hold values from -0.09375 to 0.09375
- up_routed: bfloat16 [4, 4, 3584, 512], P('pipe', 'expert', None, 'tensor'), may hold values from -0.09375 to 0.09375
- down_routed: bfloat16 [4, 4, 512, 3584], P('pipe', 'expert', 'tensor'), may hold values from -0.1875 to 0.1875
- gate_shared: bfloat16 [4, 3584, 1024], P('pipe', None, 'tensor'), may hold values from -0.09375 to 0.09375
- up_shared: bfloat16 [4, 3584, 1024], P('pipe', None, 'tensor'), may hold values from -0.09375 to 0.09375
- down_shared: bfloat16 [4, 1024, 3584], P('pipe', 'tensor'), may hold values from -0.1875 to 0.1875
Outputs:
- out_act: bfloat16 [4, 512, 3584], P('pipe', 'expert', 'tensor')
- in_grad: bfloat16 [4, 512, 3584], P('pipe', 'expert', 'tensor')
Inputs may be any that keep to these rules, and one draw needn't show every extreme that they name: `expert_ids`: each row names 8 different experts; in every section and micro-batch one expert below 2 is named by every row. `keep_mask`: 1 only where the expert named is below 2; in one block of 128 rows no expert has more than 4 kept choices, and in every section and micro-batch one expert has exactly 4 in every block. `slot_pos`: kept choices of one block naming the same expert hold different slots; 0 where keep_mask is 0.
All inputs are finite; a program needn't handle non-finite values.
Results may differ from a plain program's by a relative error of at most 0.005.
Values may be sent and summed in bfloat16 or wider, within the bound.
A program may use at most 64 MiB of HBM per device.

v0:
```python
import jax
import jax.numpy as jnp
from jax import lax
from jax.sharding import PartitionSpec as P


def passed_along(block, axis, distance):
    devices = range(lax.axis_size(axis))
    route = [((i - distance) % len(devices), i) for i in devices]
    return lax.ppermute(block, axis, route)


def swish(values):
    return values * jax.nn.sigmoid(values)


def swish_slope(values):
    logistic = jax.nn.sigmoid(values)
    return logistic * (1.0 + values * (1.0 - logistic))


def contract_last(left, right):
    return lax.dot_general(
        left, right, (((1,), (1,)), ((), ())), preferred_element_type=jnp.float32
    )


def slot_plan(choice_ids, kept_flags, slot_index, weight_levels, total_slots, capacity):
    target = jnp.where(kept_flags > 0, choice_ids * capacity + slot_index, -1)
    slots = jnp.arange(total_slots, dtype=jnp.int32)
    match = target[None] == slots[:, None, None]
    chosen = jnp.sum(match.astype(jnp.int32), axis=2)
    level = jnp.sum(jnp.where(match, weight_levels[None], 0), axis=2)
    return (chosen.astype(jnp.bfloat16), level)


def section_link(values, offset):
    return passed_along(values, "pipe", offset)


def select_rows(chosen, values):
    return jnp.dot(chosen, values, preferred_element_type=jnp.float32)


def split_level(level):
    high = (level // 64).astype(jnp.float32) / 64.0
    low = (level % 64).astype(jnp.float32) / 4096.0
    return (high.astype(jnp.bfloat16), low.astype(jnp.bfloat16))


def combine(factors, rows):
    return lax.dot_general(
        factors, rows, (((0,), (0,)), ((), ())), preferred_element_type=jnp.float32
    )


def other_sums(total, n_tensor):
    width = total.shape[1] // n_tensor
    me = lax.axis_index("tensor")
    mine = lax.dynamic_slice_in_dim(total, me * width, width, axis=1)
    for step in range(1, n_tensor):
        to = (me + step) % n_tensor
        piece = lax.dynamic_slice_in_dim(total, to * width, width, axis=1)
        mine = mine + passed_along(piece, "tensor", step)
    return mine


def expert_local(rows_in, rows_saved, rows_cot, gate_w, up_w, down_w):
    gate_pre = jnp.dot(rows_in, gate_w, preferred_element_type=jnp.float32)
    up_pre = jnp.dot(rows_in, up_w, preferred_element_type=jnp.float32)
    hidden = (swish(gate_pre) * up_pre).astype(jnp.bfloat16)
    result = jnp.dot(hidden, down_w, preferred_element_type=jnp.float32).astype(jnp.bfloat16)
    gate_back = jnp.dot(rows_saved, gate_w, preferred_element_type=jnp.float32)
    up_back = jnp.dot(rows_saved, up_w, preferred_element_type=jnp.float32)
    grad_hidden = contract_last(rows_cot, down_w)
    grad_gate = (grad_hidden * up_back * swish_slope(gate_back)).astype(jnp.bfloat16)
    grad_up = (grad_hidden * swish(gate_back)).astype(jnp.bfloat16)
    grad_rows = (contract_last(grad_gate, gate_w) + contract_last(grad_up, up_w)).astype(
        jnp.bfloat16
    )
    return (result, grad_rows)


def shared_pass(full_in, full_saved, full_cot, gate_w, up_w, down_w):
    gate_pre = jnp.dot(full_in, gate_w, preferred_element_type=jnp.float32)
    up_pre = jnp.dot(full_in, up_w, preferred_element_type=jnp.float32)
    hidden = (swish(gate_pre) * up_pre).astype(jnp.bfloat16)
    shared_out = jnp.dot(hidden, down_w, preferred_element_type=jnp.float32)
    gate_back = jnp.dot(full_saved, gate_w, preferred_element_type=jnp.float32)
    up_back = jnp.dot(full_saved, up_w, preferred_element_type=jnp.float32)
    grad_hidden = contract_last(full_cot, down_w)
    grad_gate = (grad_hidden * up_back * swish_slope(gate_back)).astype(jnp.bfloat16)
    grad_up = (grad_hidden * swish(gate_back)).astype(jnp.bfloat16)
    shared_grad = contract_last(grad_gate, gate_w) + contract_last(grad_up, up_w)
    return (shared_out, shared_grad)


def local(
    inputs_prev,
    cotangent_next,
    saved_input,
    expert_ids,
    keep_mask,
    slot_pos,
    weight_q,
    gate_routed,
    up_routed,
    down_routed,
    gate_shared,
    up_shared,
    down_shared,
):
    capacity = inputs_prev.shape[1] // 32
    n_expert = lax.axis_size("expert")
    n_tensor = lax.axis_size("tensor")
    experts_here = n_expert // 2
    slots = experts_here * capacity
    forward_in = section_link(inputs_prev[0], 1)
    backward_in = section_link(cotangent_next[0], -1)
    chosen_f, level_f = slot_plan(
        expert_ids[0, 0], keep_mask[0, 0], slot_pos[0, 0], weight_q[0, 0], slots, capacity
    )
    chosen_b, level_b = slot_plan(
        expert_ids[1, 0], keep_mask[1, 0], slot_pos[1, 0], weight_q[1, 0], slots, capacity
    )
    gate_w = gate_routed[0, 0]
    up_w = up_routed[0, 0]
    down_w = down_routed[0, 0]
    full_saved = lax.all_gather(saved_input[0], "tensor", axis=1, tiled=True)
    full_in = lax.all_gather(forward_in, "tensor", axis=1, tiled=True)
    full_cot = lax.all_gather(backward_in, "tensor", axis=1, tiled=True)
    feature_count = full_in.shape[1]
    weight_b = jnp.sum(level_b, axis=1).astype(jnp.float32) / 4096.0
    parcel = jnp.stack(
        (
            select_rows(chosen_f, full_in).astype(jnp.bfloat16),
            select_rows(chosen_b, full_saved).astype(jnp.bfloat16),
            (weight_b[:, None] * select_rows(chosen_b, full_cot)).astype(jnp.bfloat16),
        )
    ).reshape(3, experts_here, 1, capacity, feature_count)
    parcel = jnp.broadcast_to(parcel, (3, experts_here, 2, capacity, feature_count))
    parcel = parcel.reshape(3, n_expert, capacity, feature_count)
    pieces = lax.all_to_all(parcel, "expert", split_axis=1, concat_axis=1, tiled=True)
    rows = pieces.reshape(3, n_expert * capacity, feature_count)
    result, grad_rows = expert_local(rows[0], rows[1], rows[2], gate_w, up_w, down_w)
    returned = lax.all_to_all(
        jnp.stack((result, grad_rows)).reshape(2, n_expert, capacity, feature_count),
        "expert",
        split_axis=1,
        concat_axis=1,
        tiled=True,
    )
    back = returned.reshape(2, n_expert * capacity, feature_count)

    def doubled(factors):
        spread = factors.reshape(experts_here, 1, capacity, -1)
        spread = jnp.broadcast_to(spread, (experts_here, 2) + spread.shape[2:])
        return spread.reshape(n_expert * capacity, -1)

    high_f, low_f = split_level(level_f)
    factors_f = jnp.concatenate((doubled(high_f), doubled(low_f)), axis=0)
    routed_out = combine(factors_f, jnp.concatenate((back[0], back[0]), axis=0))
    routed_grad = combine(doubled(chosen_b), back[1])
    shared_out, shared_grad = shared_pass(
        full_in, full_saved, full_cot, gate_shared[0], up_shared[0], down_shared[0]
    )
    summed_out = other_sums(routed_out + shared_out, n_tensor)
    summed_grad = other_sums(routed_grad + shared_grad, n_tensor)
    return (summed_out.astype(jnp.bfloat16)[None], summed_grad.astype(jnp.bfloat16)[None])


def solution(mesh):
    return jax.shard_map(
        local,
        mesh=mesh,
        in_specs=(
            P("pipe", "expert", "tensor"),
            P("pipe", "expert", "tensor"),
            P("pipe", "expert", "tensor"),
            P(None, "pipe", "expert", None),
            P(None, "pipe", "expert", None),
            P(None, "pipe", "expert", None),
            P(None, "pipe", "expert", None),
            P("pipe", "expert", None, "tensor"),
            P("pipe", "expert", None, "tensor"),
            P("pipe", "expert", "tensor", None),
            P("pipe", None, "tensor"),
            P("pipe", None, "tensor"),
            P("pipe", "tensor", None),
        ),
        out_specs=(P("pipe", "expert", "tensor"), P("pipe", "expert", "tensor")),
        check_vma=False,
    )
```

profile of v0, /device:TPU:0, one launch (start us, length us, event | category | flops | bytes accessed | tf_op | source)
XLA Modules:
  0.0 99.7 jit_solution(14145739943017148776)
XLA Ops:
  0.6 0.0 copy-start
  0.6 5.1 %collective-permute-start.1 = (bf16[128,1792]{1,0:T(8,128)(2,1)}, bf16[128,1792]{1,0:T(8,128)(2,1)}, u32[]{:S(2)}, u32[]{:S(2)}) collective-permute-start(bf16[128,1792]{1,0:T(8,128)(2,1)} %bitcast.127), channel_id=1, source_target_pairs={{8,0},{16,8},{24,16},{0,24},{9,1},{17,9},{25,17},{1,25},{10,2},{18... | collective-permute-start | bytes 1376264 | tf_op jit(solution)/shard_map/ppermute | solution.py:10
  5.8 0.8 slice_bitcast_fusion.1
  6.6 0.2 select_reduce_fusion
  6.8 2.7 %all-gather = bf16[1,128,3584]{2,1,0:T(8,128)(2,1)S(1)} all-gather(bf16[1,128,1792]{2,1,0:T(8,128)(2,1)} %param.15), channel_id=2, replica_groups=mesh['pipe'=4,'expert'=4,'tensor'=2] {'tensor'}, dimensions={2}, use_global_device_ids=true | all-gather | bytes 1376256 | tf_op jit(solution)/shard_map/all_gather | solution.py:129
  9.6 0.2 convolution_convert_fusion.1
  9.8 2.7 %fusion.13 = f32[128,512]{1,0:T(8,128)S(1)} fusion(bf16[1,3584,512]{2,1,0:T(8,128)(2,1)} %param.23, bf16[1,128,3584]{2,1,0:T(8,128)(2,1)S(1)} %all-gather), kind=kOutput, calls=%fused_computation.20 | convolution fusion | flops 469762048 | bytes 4849664 | tf_op jit(solution)/shard_map/dot_general | solution.py:89
  12.5 4.5 %collective-permute-done.1 = bf16[128,1792]{1,0:T(8,128)(2,1)} collective-permute-done((bf16[128,1792]{1,0:T(8,128)(2,1)}, bf16[128,1792]{1,0:T(8,128)(2,1)}, u32[]{:S(2)}, u32[]{:S(2)}) %collective-permute-start.1) | collective-permute-done | bytes 458784 | tf_op jit(solution)/shard_map/ppermute | solution.py:10
  17.0 2.7 %all_gather.11 = bf16[128,3584]{1,0:T(8,128)(2,1)S(1)} all-gather(bf16[128,1792]{1,0:T(8,128)(2,1)} %collective-permute-done.1), channel_id=1, replica_groups=mesh['pipe'=4,'expert'=4,'tensor'=2] {'tensor'}, dimensions={1}, use_global_device_ids=true | all-gather | bytes 1376256 | tf_op jit(solution)/shard_map/all_gather | solution.py:131
  19.7 0.9 fusion.2
  20.6 1.5 %stack.23 = bf16[1,2,1,4,3584]{4,3,1,2,0:T(4,128)(2,1)} reshape(bf16[8,3584]{1,0:T(8,128)(2,1)} %fusion.2) | data formatting | bytes 114688 | tf_op jit(solution)/shard_map/stack | solution.py:134
  22.1 4.4 %collective-permute-done = bf16[128,1792]{1,0:T(8,128)(2,1)S(1)} collective-permute-done((bf16[128,1792]{1,0:T(8,128)(2,1)}, bf16[128,1792]{1,0:T(8,128)(2,1)S(1)}, u32[]{:S(2)}, u32[]{:S(2)}) %collective-permute-start) | collective-permute-done | bytes 458784 | tf_op jit(solution)/shard_map/ppermute | solution.py:10
  26.5 2.5 %all_gather.9 = bf16[128,3584]{1,0:T(8,128)(2,1)S(1)} all-gather(bf16[128,1792]{1,0:T(8,128)(2,1)S(1)} %collective-permute-done), channel_id=1, replica_groups=mesh['pipe'=4,'expert'=4,'tensor'=2] {'tensor'}, dimensions={1}, use_global_device_ids=true | all-gather | bytes 1376256 | tf_op jit(solution)/shard_map/all_gather | solution.py:130
  29.0 0.2 convolution_convert_fusion.2
  29.2 1.0 maximum_bitcast_fusion
  30.2 0.1 copy.26
  30.2 0.8 broadcast_in_dim.69
  31.1 4.1 %all-to-all-start = ((bf16[3,4,4,3584]{3,2,0,1:T(4,128)(2,1)}), bf16[3,4,4,3584]{3,2,0,1:T(4,128)(2,1)}, u32[]{:S(2)}, u32[]{:S(2)}) async-start(bf16[3,4,4,3584]{3,2,0,1:T(4,128)(2,1)} %bitcast.11), calls=%async_computation | async-start | bytes 688128 | tf_op jit(solution)/shard_map/all_to_all | solution.py:143
  35.2 3.6 %fusion.3 = f32[128,512]{1,0:T(8,128)S(1)} fusion(bf16[128,3584]{1,0:T(8,128)(2,1)} %copy-done.3, bf16[1,512,3584]{2,1,0:T(8,128)(2,1)} %param.25), kind=kOutput, calls=%fused_computation.10 | convolution fusion | flops 469762048 | bytes 4849664 | tf_op jit(solution)/shard_map/dot_general | solution.py:23
  38.8 6.6 %fusion.11 = f32[128,3584]{1,0:T(8,128)} fusion(bf16[1,3584,512]{2,1,0:T(8,128)(2,1)} %param.23, f32[128,512]{1,0:T(8,128)S(1)} %fusion.3, bf16[1,3584,512]{2,1,0:T(8,128)(2,1)} %param.24, bf16[1,128,3584]{2,1,0:T(8,128)(2,1)} %copy-done.2, f32[128,512]{1,0:T(8,128)S(1)} %fusion.13), kind=kOutput, calls=%fused_computation.18 | convolution fusion | flops 940179456 | bytes 10616832 | tf_op jit(solution)/shard_map/dot_general | solution.py:23
  45.4 1.8 %fusion.112 = (bf16[1,4,4,3584]{3,2,0,1:T(4,128)(2,1)}, bf16[1,4,4,3584]{3,2,0,1:T(4,128)(2,1)S(1)}, bf16[1,4,4,3584]{3,2,0,1:T(4,128)(2,1)S(1)}) fusion(bf16[3,4,4,3584]{3,2,0,1:T(4,128)(2,1)} %all-to-all-done), kind=kLoop, calls=%fused_computation.123 | loop fusion | bytes 688128 | tf_op jit(solution)/shard_map/slice | solution.py:145
  47.1 0.7 squeeze.56
  47.9 2.2 %fusion.17 = f32[16,256]{1,0:T(8,128)S(1)} fusion(bf16[16,3584]{1,0:T(8,128)(2,1)} %squeeze.56, bf16[1,1,256,3584]{3,2,1,0:T(8,128)(2,1)} %param.22), kind=kOutput, calls=%fused_computation.24 | convolution fusion | flops 29360128 | bytes 1966080 | tf_op jit(solution)/shard_map/dot_general | solution.py:23
  50.1 0.4 fusion.27
  50.5 3.5 %fusion.25 = f32[16,3584]{1,0:T(8,128)} fusion(bf16[1,1,3584,256]{3,2,1,0:T(8,128)(2,1)} %param.20, f32[16,256]{1,0:T(8,128)S(1)} %fusion.17, bf16[16,3584]{1,0:T(8,128)(2,1)S(1)} %squeeze.57, bf16[1,1,3584,256]{3,2,1,0:T(8,128)(2,1)S(1)} %copy-done, f32[16,256]{1,0:T(8,128)S(1)} %fusion.27), kind=kOutput, calls=%fused_computation.32 | convolution fusion | flops 58761216 | bytes 4046848 | tf_op jit(solution)/shard_map/dot_general | solution.py:23
  54.0 1.5 %fusion.1 = bf16[16,3584]{1,0:T(8,128)(2,1)S(1)} fusion(f32[16,3584]{1,0:T(8,128)} %fusion.25, bf16[1,1,3584,256]{3,2,1,0:T(8,128)(2,1)S(1)} %copy-done, f32[16,256]{1,0:T(8,128)S(1)} %fusion.17, f32[16,256]{1,0:T(8,128)S(1)} %fusion.27), kind=kOutput, calls=%fused_computation.4 | convolution fusion | flops 29499392 | bytes 2211840 | tf_op jit(solution)/shard_map/dot_general | solution.py:23
  55.5 0.9 squeeze.52
  56.5 1.8 %fusion.29 = f32[16,256]{1,0:T(8,128)S(1)} fusion(bf16[16,3584]{1,0:T(8,128)(2,1)S(1)} %squeeze.52, bf16[1,1,3584,256]{3,2,1,0:T(8,128)(2,1)} %param.20), kind=kOutput, calls=%fused_computation.36 | convolution fusion | flops 29360128 | bytes 1966080 | tf_op jit(solution)/shard_map/dot_general | solution.py:69
  58.3 3.3 %convolution_convert_fusion = bf16[16,3584]{1,0:T(8,128)(2,1)} fusion(bf16[1,1,256,3584]{3,2,1,0:T(8,128)(2,1)} %param.22, bf16[16,3584]{1,0:T(8,128)(2,1)S(1)} %squeeze.52, bf16[1,1,3584,256]{3,2,1,0:T(8,128)(2,1)S(1)} %copy-done, f32[16,256]{1,0:T(8,128)S(1)} %fusion.29), kind=kOutput, calls=%fused_computation.5 | convolution fusion | flops 58802176 | bytes 3915776 | tf_op jit(solution)/shard_map/dot_general | solution.py:72
  61.6 0.9 stack.25
  62.5 0.8 pad_maximum_fusion
  63.4 4.1 %all-to-all-start.1 = ((bf16[2,4,4,3584]{3,2,0,1:T(4,128)(2,1)}), bf16[2,4,4,3584]{3,2,0,1:T(4,128)(2,1)}, u32[]{:S(2)}, u32[]{:S(2)}) async-start(bf16[2,4,4,3584]{3,2,0,1:T(4,128)(2,1)} %pad_maximum_fusion), calls=%async_computation.1 | async-start | bytes 458752 | tf_op jit(solution)/shard_map/all_to_all | solution.py:146
  67.5 2.7 %fusion.9 = f32[128,512]{1,0:T(8,128)S(1)} fusion(bf16[128,3584]{1,0:T(8,128)(2,1)S(1)} %all_gather.9, bf16[1,3584,512]{2,1,0:T(8,128)(2,1)} %param.24), kind=kOutput, calls=%fused_computation.16 | convolution fusion | flops 469762048 | bytes 4849664 | tf_op jit(solution)/shard_map/dot_general | solution.py:86
  70.2 3.0 %all-to-all-done.1 = bf16[2,4,4,3584]{3,2,0,1:T(4,128)(2,1)} async-done(((bf16[2,4,4,3584]{3,2,0,1:T(4,128)(2,1)}), bf16[2,4,4,3584]{3,2,0,1:T(4,128)(2,1)}, u32[]{:S(2)}, u32[]{:S(2)}) %all-to-all-start.1) | async-done | bytes 229408 | tf_op jit(solution)/shard_map/all_to_all | solution.py:146
  73.2 1.7 %fusion.113 = (bf16[1,4,4,3584]{3,2,0,1:T(4,128)(2,1)}, bf16[1,4,4,3584]{3,2,0,1:T(4,128)(2,1)}) fusion(bf16[2,4,4,3584]{3,2,0,1:T(4,128)(2,1)} %all-to-all-done.1), kind=kLoop, calls=%fused_computation.124 | loop fusion | bytes 458752 | tf_op jit(solution)/shard_map/slice | solution.py:163
  74.9 1.6 %squeeze.58 = bf16[16,3584]{1,0:T(8,128)(2,1)} reshape(bf16[1,4,4,3584]{3,2,0,1:T(4,128)(2,1)} %get-tuple-element.10) | data formatting | bytes 229376 | tf_op jit(solution)/shard_map/squeeze | solution.py:162
  76.5 2.6 %fusion.71 = f32[128,3584]{1,0:T(8,128)} fusion(bf16[16,3584]{1,0:T(8,128)(2,1)} %squeeze.58, bf16[16,128]{1,0:T(8,128)(2,1)S(1)} %bitcast.123, bf16[16,128]{1,0:T(8,128)(2,1)S(1)} %bitcast.124), kind=kOutput, calls=%fused_computation.61 | convolution fusion | flops 29835264 | bytes 1957888 | tf_op jit(solution)/shard_map/dot_general | solution.py:52
  79.1 6.2 %convolution_add_fusion.1 = f32[128,3584]{1,0:T(8,128)} fusion(f32[128,3584]{1,0:T(8,128)} %fusion.71, bf16[1,512,3584]{2,1,0:T(8,128)(2,1)} %param.25, f32[128,512]{1,0:T(8,128)S(1)} %fusion.9, bf16[128,3584]{1,0:T(8,128)(2,1)S(1)} %all_gather.9, bf16[1,3584,512]{2,1,0:T(8,128)(2,1)} %param.23), kind=kOutput, calls=%fused_computation.2 | convolution fusion | flops 940376064 | bytes 12189696 | tf_op jit(solution)/shard_map/dot_general | solution.py:88
  85.3 2.2 %constant_dynamic-slice_fusion = f32[128,1792]{1,0:T(8,128)} fusion(f32[128,3584]{1,0:T(8,128)} %convolution_add_fusion.1, s32[]{:T(128)S(6)} %select_n.74), kind=kLoop, calls=%fused_computation.113 | loop fusion | bytes 1835012 | tf_op jit(solution)/shard_map/dynamic_slice | solution.py:63
  87.6 0.4 fusion.114
  88.0 1.1 %copy-done.6 = f32[128,3584]{1,0:T(8,128)S(1)} copy-done((f32[128,3584]{1,0:T(8,128)S(1)}, f32[128,3584]{1,0:T(8,128)}, u32[]{:S(2)}) %copy-start.6) | copy-done | bytes 1835032
  89.1 3.4 %fusion = f32[128,3584]{1,0:T(8,128)S(1)} fusion(f32[128,3584]{1,0:T(8,128)S(1)} %fusion.114, f32[128,3584]{1,0:T(8,128)S(1)} %copy-done.6, bf16[1,3584,512]{2,1,0:T(8,128)(2,1)} %param.24, f32[128,512]{1,0:T(8,128)S(1)} %fusion.3, f32[128,512]{1,0:T(8,128)S(1)} %fusion.13), kind=kOutput, calls=%fused_computation.1 | convolution fusion | flops 471072768 | bytes 9699328 | tf_op jit(solution)/shard_map/dot_general | solution.py:23
  92.5 1.3 %copy-done.4 = f32[128,3584]{1,0:T(8,128)} copy-done((f32[128,3584]{1,0:T(8,128)}, f32[128,3584]{1,0:T(8,128)S(1)}, u32[]{:S(2)}) %copy-start.4) | copy-done | bytes 1835032
  93.7 1.0 %constant_dynamic-slice_fusion.1 = f32[128,1792]{1,0:T(8,128)} fusion(f32[128,3584]{1,0:T(8,128)S(1)} %fusion, s32[]{:T(128)S(6)} %select_n.74), kind=kLoop, calls=%fused_computation.114 | loop fusion | bytes 1835012 | tf_op jit(solution)/shard_map/dynamic_slice | solution.py:63
  94.7 0.5 collective-permute-start.3
  95.2 2.2 %fusion.65 = bf16[1,128,1792]{2,1,0:T(8,128)(2,1)} fusion(f32[128,1792]{1,0:T(8,128)S(1)} %collective-permute-done.2, f32[128,3584]{1,0:T(8,128)} %convolution_add_fusion.1, s32[]{:T(128)S(6)} %select_n.72), kind=kLoop, calls=%fused_computation.51 | loop fusion | flops 458752 | bytes 2293764 | tf_op jit(solution)/shard_map/broadcast_in_dim | solution.py:169
  97.4 0.3 collective-permute-done.3
  97.7 2.0 %fusion.66 = bf16[1,128,1792]{2,1,0:T(8,128)(2,1)} fusion(f32[128,1792]{1,0:T(8,128)} %collective-permute-done.3, f32[128,3584]{1,0:T(8,128)S(1)} %copy-done.5, s32[]{:T(128)S(6)} %select_n.72), kind=kLoop, calls=%fused_computation.52 | loop fusion | flops 458752 | bytes 2293764 | tf_op jit(solution)/shard_map/broadcast_in_dim | solution.py:169
  (29 shorter events, 0.3 us)
Async XLA Ops:
  0.6 49.9 %copy-start = (bf16[1,1,3584,256]{3,2,1,0:T(8,128)(2,1)S(1)}, bf16[1,1,3584,256]{3,2,1,0:T(8,128)(2,1)}, u32[]{:S(2)}) copy-start(bf16[1,1,3584,256]{3,2,1,0:T(8,128)(2,1)} %param.21) | copy-start | bytes 5505028
  0.6 16.4 %collective-permute-start.1 = (bf16[128,1792]{1,0:T(8,128)(2,1)}, bf16[128,1792]{1,0:T(8,128)(2,1)}, u32[]{:S(2)}, u32[]{:S(2)}) collective-permute-start(bf16[128,1792]{1,0:T(8,128)(2,1)} %bitcast.127), channel_id=1, source_target_pairs={{8,0},{16,8},{24,16},{0,24},{9,1},{17,9},{25,17},{1,25},{10,2},{18... | collective-permute-start | bytes 1376264 | tf_op jit(solution)/shard_map/ppermute | solution.py:10
  5.8 20.7 %collective-permute-start = (bf16[128,1792]{1,0:T(8,128)(2,1)}, bf16[128,1792]{1,0:T(8,128)(2,1)S(1)}, u32[]{:S(2)}, u32[]{:S(2)}) collective-permute-start(bf16[128,1792]{1,0:T(8,128)(2,1)} %bitcast.128), channel_id=1, source_target_pairs={{24,0},{0,8},{8,16},{16,24},{25,1},{1,9},{9,17},{17,25},{26,2},{2,... | collective-permute-start | bytes 1376264 | tf_op jit(solution)/shard_map/ppermute | solution.py:10
  9.5 3.0 %copy-start.2 = (bf16[1,128,3584]{2,1,0:T(8,128)(2,1)}, bf16[1,128,3584]{2,1,0:T(8,128)(2,1)S(1)}, u32[]{:S(2)}) copy-start(bf16[1,128,3584]{2,1,0:T(8,128)(2,1)S(1)} %all-gather) | copy-start | bytes 2752516
  19.7 2.4 %copy-start.3 = (bf16[128,3584]{1,0:T(8,128)(2,1)}, bf16[128,3584]{1,0:T(8,128)(2,1)S(1)}, u32[]{:S(2)}) copy-start(bf16[128,3584]{1,0:T(8,128)(2,1)S(1)} %all_gather.11) | copy-start | bytes 2752516
  31.1 14.3 %all-to-all-start = ((bf16[3,4,4,3584]{3,2,0,1:T(4,128)(2,1)}), bf16[3,4,4,3584]{3,2,0,1:T(4,128)(2,1)}, u32[]{:S(2)}, u32[]{:S(2)}) async-start(bf16[3,4,4,3584]{3,2,0,1:T(4,128)(2,1)} %bitcast.11), calls=%async_computation | async-start | bytes 688128 | tf_op jit(solution)/shard_map/all_to_all | solution.py:143
  47.8 2.3 %copy-start.1 = (bf16[1,1,3584,256]{3,2,1,0:T(8,128)(2,1)S(1)}, bf16[1,1,3584,256]{3,2,1,0:T(8,128)(2,1)}, u32[]{:S(2)}) copy-start(bf16[1,1,3584,256]{3,2,1,0:T(8,128)(2,1)} %param.20) | copy-start | bytes 5505028
  63.4 9.8 %all-to-all-start.1 = ((bf16[2,4,4,3584]{3,2,0,1:T(4,128)(2,1)}), bf16[2,4,4,3584]{3,2,0,1:T(4,128)(2,1)}, u32[]{:S(2)}, u32[]{:S(2)}) async-start(bf16[2,4,4,3584]{3,2,0,1:T(4,128)(2,1)} %pad_maximum_fusion), calls=%async_computation.1 | async-start | bytes 458752 | tf_op jit(solution)/shard_map/all_to_all | solution.py:146
  85.3 2.2 %copy-start.7 = (bf16[1,4,4,3584]{3,2,0,1:T(4,128)(2,1)S(1)}, bf16[1,4,4,3584]{3,2,0,1:T(4,128)(2,1)}, u32[]{:S(2)}) copy-start(bf16[1,4,4,3584]{3,2,0,1:T(4,128)(2,1)} %get-tuple-element.9) | copy-start | bytes 344068
  87.5 7.7 %collective-permute-start.2 = (f32[128,1792]{1,0:T(8,128)}, f32[128,1792]{1,0:T(8,128)S(1)}, u32[]{:S(2)}, u32[]{:S(2)}) collective-permute-start(f32[128,1792]{1,0:T(8,128)} %constant_dynamic-slice_fusion), channel_id=1, source_target_pairs={{1,0},{0,1},{3,2},{2,3},{5,4},{4,5},{7,6},{6,7},{9,8},{8,9},{11,10... | collective-permute-start | bytes 2752520 | tf_op jit(solution)/shard_map/ppermute | solution.py:10
  87.6 1.5 %copy-start.6 = (f32[128,3584]{1,0:T(8,128)S(1)}, f32[128,3584]{1,0:T(8,128)}, u32[]{:S(2)}) copy-start(f32[128,3584]{1,0:T(8,128)} %fusion.11) | copy-start | bytes 5505028
  92.4 1.3 %copy-start.4 = (f32[128,3584]{1,0:T(8,128)}, f32[128,3584]{1,0:T(8,128)S(1)}, u32[]{:S(2)}) copy-start(f32[128,3584]{1,0:T(8,128)S(1)} %fusion) | copy-start | bytes 5505028
  94.7 2.9 %collective-permute-start.3 = (f32[128,1792]{1,0:T(8,128)}, f32[128,1792]{1,0:T(8,128)}, u32[]{:S(2)}, u32[]{:S(2)}) collective-permute-start(f32[128,1792]{1,0:T(8,128)} %constant_dynamic-slice_fusion.1), channel_id=1, source_target_pairs={{1,0},{0,1},{3,2},{2,3},{5,4},{4,5},{7,6},{6,7},{9,8},{8,9},{11,10... | collective-permute-start | bytes 2752520 | tf_op jit(solution)/shard_map/ppermute | solution.py:10
  95.2 2.4 %copy-start.5 = (f32[128,3584]{1,0:T(8,128)S(1)}, f32[128,3584]{1,0:T(8,128)}, u32[]{:S(2)}) copy-start(f32[128,3584]{1,0:T(8,128)} %copy-done.4) | copy-start | bytes 5505028
where the time goes:
time: 101 us; the launch traced here: 99.7 us
  matrix products  42.3 us (42%)
  local copies, waits for them, and re-layouts  15.7 us (16%)
  starting transfers between devices  13.9 us (14%)
  waiting for transfers between devices  12.2 us (12%)
  blocking collectives  7.79 us (8%)
  other arithmetic  7.08 us (7%)
    dot_general x6, matrix products, contract_last(): lax.dot_general(left, right, (((1,), (1,)), ((), ())), preferred_element_...  20.8 us
    ppermute x4, waiting for transfers between devices, passed_along(): return lax.ppermute(block, axis, route)  9.2 us
    dot_general x1, matrix products, shared_pass(): shared_out = jnp.dot(hidden, down_w, preferred_element_type=jnp.float32)  6.2 us
    ppermute x4, starting transfers between devices, passed_along(): return lax.ppermute(block, axis, route)  5.64 us
    all_to_all x1, starting transfers between devices, local(): lax.all_to_all(jnp.stack((result, grad_rows)).reshape(2, n_expert, capaci...  4.14 us
    all_to_all x1, starting transfers between devices, local(): lax.all_to_all(parcel, 'expert', split_axis=1, concat_axis=1, tiled=True)  4.1 us
    dot_general x1, matrix products, expert_local(): jnp.dot(hidden, down_w, preferred_element_type=jnp.float32)  3.3 us
    dynamic_slice x2, local copies, waits for them, and re-layouts, other_sums(): piece = lax.dynamic_slice_in_dim(total, to * width, width, axis=1)  3.22 us
  transfers between devices with their start and end apart: 6, of which 4 were waited for; matrix products, arithmetic and copies ran while one was open for 26% of the time, Pallas kernels for 0%

commit v1 on v0

--- a/solution.py
+++ b/solution.py
@@ -127,8 +127,12 @@
     up_w = up_routed[0, 0]
     down_w = down_routed[0, 0]
     full_saved = lax.all_gather(saved_input[0], "tensor", axis=1, tiled=True)
-    full_in = lax.all_gather(forward_in, "tensor", axis=1, tiled=True)
-    full_cot = lax.all_gather(backward_in, "tensor", axis=1, tiled=True)
+    feed_column = lambda x_local, panel: jnp.split(
+        lax.all_gather(jnp.concatenate([x_local, panel], 0), "tensor", axis=1, tiled=True),
+        [x_local.shape[0]],
+        0,
+    )
+    full_in, full_cot = feed_column(forward_in, backward_in)
     feature_count = full_in.shape[1]
     weight_b = jnp.sum(level_b, axis=1).astype(jnp.float32) / 4096.0
     parcel = jnp.stack(

time: 101 us -> 114 us (1.13)
  waiting for transfers between devices: 12.2 us -> 27.1 us
  between operations: 0.82 us -> 14.3 us
  local copies, waits for them, and re-layouts: 15.7 us -> 7.08 us
  blocking collectives: 7.79 us -> 2.46 us
    ppermute x4, waiting for transfers between devices: 9.2 us -> 20.2 us  [passed_along(): return lax.ppermute(block, axis, route)]
    all_gather x2 -> x0, blocking collectives: 5.11 us -> none  [the longest x1 2.66 us: local(): full_cot = lax.all_gather(backward_in, 'tensor', axis=1, tiled=True)]
    all_gather x0 -> x1, waiting for transfers between devices: none -> 4.5 us  [local(): lax.all_gather(jnp.concatenate([x_local, panel], 0), 'tensor', axis=1, ti...]
    dot_general x6, matrix products: 20.8 us -> 18.2 us  [contract_last(): lax.dot_general(left, right, (((1,), (1,)), ((), ())), preferred_element_...]
    dot_general x3, matrix products: 1.35 us -> 3.02 us  [select_rows(): return jnp.dot(chosen, values, preferred_element_type=jnp.float32)]
    slice x1, local copies, waits for them, and re-layouts: 1.72 us -> 0.08 us  [local(): routed_grad = combine(doubled(chosen_b), back[1])]
    squeeze x1, local copies, waits for them, and re-layouts: 1.57 us -> 0.03 us  [local(): routed_out = combine(factors_f, jnp.concatenate((back[0], back[0]), axis=0))]
    dot_general x1, matrix products: 0.38 us -> 1.85 us  [expert_local(): gate_back = jnp.dot(rows_saved, gate_w, preferred_element_type=jnp.float32)]
  transfers between devices with their start and end apart: 6 -> 7, of which waited for: 4 -> 5; matrix products, arithmetic and copies ran while one was open for 26% -> 20% of each run, Pallas kernels for 0% -> 0%
where the time goes in v1:
time: 114 us; the launch traced here: 113 us
  matrix products  41.7 us (37%)
  waiting for transfers between devices  27.1 us (24%)
  between operations  14.3 us (13%)
  starting transfers between devices  14 us (12%)
  local copies, waits for them, and re-layouts  7.08 us (6%)
  other arithmetic  6.46 us (6%)
  blocking collectives  2.46 us (2%)
    ppermute x4, waiting for transfers between devices, passed_along(): return lax.ppermute(block, axis, route)  20.2 us
    dot_general x6, matrix products, contract_last(): lax.dot_general(left, right, (((1,), (1,)), ((), ())), preferred_element_...  18.2 us
    dot_general x1, matrix products, shared_pass(): shared_out = jnp.dot(hidden, down_w, preferred_element_type=jnp.float32)  6.43 us
    ppermute x4, starting transfers between devices, passed_along(): return lax.ppermute(block, axis, route)  5.71 us
    all_gather x1, waiting for transfers between devices, local(): lax.all_gather(jnp.concatenate([x_local, panel], 0), 'tensor', axis=1, ti...  4.5 us
    all_to_all x1, starting transfers between devices, local(): lax.all_to_all(jnp.stack((result, grad_rows)).reshape(2, n_expert, capaci...  4.13 us
    all_to_all x1, starting transfers between devices, local(): lax.all_to_all(parcel, 'expert', split_axis=1, concat_axis=1, tiled=True)  4.1 us
    dynamic_slice x2, local copies, waits for them, and re-layouts, other_sums(): piece = lax.dynamic_slice_in_dim(total, to * width, width, axis=1)  3.31 us
  transfers between devices with their start and end apart: 7, of which 5 were waited for; matrix products, arithmetic and copies ran while one was open for 20% of the time, Pallas kernels for 0%

profile of v1, /device:TPU:0, one launch (start us, length us, event | category | flops | bytes accessed | tf_op | source)
XLA Modules:
  0.0 113.1 jit_solution(10842644721731530854)
XLA Ops:
  7.2 0.0 copy-start
  7.2 0.0 all-gather.3.cloned.1.call-start
  7.3 3.1 %collective-permute-start = (bf16[128,1792]{1,0:T(8,128)(2,1)}, bf16[128,1792]{1,0:T(8,128)(2,1)S(1)}, u32[]{:S(2)}, u32[]{:S(2)}) collective-permute-start(bf16[128,1792]{1,0:T(8,128)(2,1)} %bitcast.124), channel_id=1, source_target_pairs={{24,0},{0,8},{8,16},{16,24},{25,1},{1,9},{9,17},{17,25},{26,2},{2,... | collective-permute-start | bytes 1376264 | tf_op jit(solution)/shard_map/ppermute | solution.py:10
  10.4 2.1 %collective-permute-start.1 = (bf16[128,1792]{1,0:T(8,128)(2,1)}, bf16[128,1792]{1,0:T(8,128)(2,1)S(1)}, u32[]{:S(2)}, u32[]{:S(2)}) collective-permute-start(bf16[128,1792]{1,0:T(8,128)(2,1)} %bitcast.125), channel_id=1, source_target_pairs={{8,0},{16,8},{24,16},{0,24},{9,1},{17,9},{25,17},{1,25},{10,2},{18... | collective-permute-start | bytes 1376264 | tf_op jit(solution)/shard_map/ppermute | solution.py:10
  12.5 11.6 %collective-permute-done = bf16[128,1792]{1,0:T(8,128)(2,1)S(1)} collective-permute-done((bf16[128,1792]{1,0:T(8,128)(2,1)}, bf16[128,1792]{1,0:T(8,128)(2,1)S(1)}, u32[]{:S(2)}, u32[]{:S(2)}) %collective-permute-start) | collective-permute-done | bytes 458784 | tf_op jit(solution)/shard_map/ppermute | solution.py:10
  24.0 8.4 %collective-permute-done.1 = bf16[128,1792]{1,0:T(8,128)(2,1)S(1)} collective-permute-done((bf16[128,1792]{1,0:T(8,128)(2,1)}, bf16[128,1792]{1,0:T(8,128)(2,1)S(1)}, u32[]{:S(2)}, u32[]{:S(2)}) %collective-permute-start.1) | collective-permute-done | bytes 458784 | tf_op jit(solution)/shard_map/ppermute | solution.py:10
  32.4 1.0 pad_maximum_fusion
  33.4 0.0 all-gather.3.cloned.1.call-update
  33.5 0.2 select_reduce_fusion
  33.7 0.0 copy-done.4
  33.7 2.5 %all-gather = bf16[1,128,3584]{2,1,0:T(8,128)(2,1)S(1)} all-gather(bf16[1,128,1792]{2,1,0:T(8,128)(2,1)S(1)} %copy-done.4), channel_id=2, replica_groups=mesh['pipe'=4,'expert'=4,'tensor'=2] {'tensor'}, dimensions={2}, use_global_device_ids=true | all-gather | bytes 1376256 | tf_op jit(solution)/shard_map/all_gather | solution.py:129
  36.2 0.2 convolution_convert_fusion.1
  36.5 2.7 %fusion.13 = f32[128,512]{1,0:T(8,128)S(1)} fusion(bf16[1,3584,512]{2,1,0:T(8,128)(2,1)} %param.23, bf16[1,128,3584]{2,1,0:T(8,128)(2,1)S(1)} %all-gather), kind=kOutput, calls=%fused_computation.20 | convolution fusion | flops 469762048 | bytes 4849664 | tf_op jit(solution)/shard_map/dot_general | solution.py:89
  39.2 4.5 %all-gather.3.cloned.1.call-done = bf16[256,3584]{1,0:T(8,128)(2,1)} async-done(((bf16[256,1792]{1,0:T(8,128)(2,1)}), bf16[256,3584]{1,0:T(8,128)(2,1)}) %all-gather.3.cloned.1.call-update) | async-done | bytes 1835024 | tf_op jit(solution)/shard_map/all_gather | solution.py:131
  43.7 1.4 %convolution_convert_fusion.2 = bf16[8,3584]{1,0:T(8,128)(2,1)S(1)} fusion(bf16[256,3584]{1,0:T(8,128)(2,1)} %all-gather.3.cloned.1.call-done, s32[8,128]{1,0:T(8,128)S(1)} %get-tuple-element.3), kind=kOutput, calls=%fused_computation.9 | convolution fusion | flops 7369728 | bytes 978944 | tf_op jit(solution)/shard_map/dot_general | solution.py:42
  45.2 1.4 %fusion.2 = bf16[8,3584]{1,0:T(8,128)(2,1)S(1)} fusion(bf16[8,128]{1,0:T(8,128)(2,1)S(1)} %convert_element_type.101, bf16[256,3584]{1,0:T(8,128)(2,1)} %all-gather.3.cloned.1.call-done, f32[8]{0:T(128)S(1)} %convert_multiply_fusion), kind=kOutput, calls=%fused_computation.7 | convolution fusion | flops 7397376 | bytes 976928 | tf_op jit(solution)/shard_map/dot_general | solution.py:42
  46.6 0.1 maximum_bitcast_fusion
  46.7 0.1 copy.26
  46.8 0.8 broadcast_in_dim.69
  47.6 4.1 %all-to-all-start = ((bf16[3,4,4,3584]{3,2,0,1:T(4,128)(2,1)}), bf16[3,4,4,3584]{3,2,0,1:T(4,128)(2,1)}, u32[]{:S(2)}, u32[]{:S(2)}) async-start(bf16[3,4,4,3584]{3,2,0,1:T(4,128)(2,1)} %bitcast.11), calls=%async_computation | async-start | bytes 688128 | tf_op jit(solution)/shard_map/all_to_all | solution.py:147
  51.7 3.6 %fusion.3 = f32[128,512]{1,0:T(8,128)S(1)} fusion(bf16[1,512,3584]{2,1,0:T(8,128)(2,1)} %param.25, bf16[256,3584]{1,0:T(8,128)(2,1)} %all-gather.3.cloned.1.call-done), kind=kOutput, calls=%fused_computation.10 | convolution fusion | flops 469762048 | bytes 4849664 | tf_op jit(solution)/shard_map/dot_general | solution.py:23
  55.3 6.3 %fusion.11 = f32[128,3584]{1,0:T(8,128)} fusion(bf16[1,3584,512]{2,1,0:T(8,128)(2,1)} %param.23, f32[128,512]{1,0:T(8,128)S(1)} %fusion.3, bf16[1,3584,512]{2,1,0:T(8,128)(2,1)} %param.24, bf16[1,128,3584]{2,1,0:T(8,128)(2,1)S(1)} %all-gather, f32[128,512]{1,0:T(8,128)S(1)} %fusion.13), kind=kOutput, calls=%fused_computation.18 | convolution fusion | flops 940179456 | bytes 10616832 | tf_op jit(solution)/shard_map/dot_general | solution.py:23
  61.6 0.0 all-to-all-done
  61.6 1.1 fusion.127
  62.8 1.8 %fusion.29 = f32[16,256]{1,0:T(8,128)S(1)} fusion(bf16[16,3584]{1,0:T(8,128)(2,1)S(1)} %squeeze.52, bf16[1,1,3584,256]{3,2,1,0:T(8,128)(2,1)} %param.20), kind=kOutput, calls=%fused_computation.36 | convolution fusion | flops 29360128 | bytes 1966080 | tf_op jit(solution)/shard_map/dot_general | solution.py:69
  64.6 2.6 %convolution_convert_fusion = bf16[16,3584]{1,0:T(8,128)(2,1)S(1)} fusion(bf16[1,1,256,3584]{3,2,1,0:T(8,128)(2,1)} %param.22, bf16[16,3584]{1,0:T(8,128)(2,1)S(1)} %squeeze.52, bf16[1,1,3584,256]{3,2,1,0:T(8,128)(2,1)S(1)} %copy-done, f32[16,256]{1,0:T(8,128)S(1)} %fusion.29), kind=kOutput, calls=%fused_computation.5 | convolution fusion | flops 58802176 | bytes 3915776 | tf_op jit(solution)/shard_map/dot_general | solution.py:72
  67.4 1.8 %fusion.27 = f32[16,256]{1,0:T(8,128)S(1)} fusion(bf16[16,3584]{1,0:T(8,128)(2,1)S(1)} %squeeze.57, bf16[1,1,3584,256]{3,2,1,0:T(8,128)(2,1)} %param.20), kind=kOutput, calls=%fused_computation.34 | convolution fusion | flops 29360128 | bytes 1966080 | tf_op jit(solution)/shard_map/dot_general | solution.py:73
  69.3 2.1 %fusion.17 = f32[16,256]{1,0:T(8,128)S(1)} fusion(bf16[16,3584]{1,0:T(8,128)(2,1)S(1)} %squeeze.56, bf16[1,1,256,3584]{3,2,1,0:T(8,128)(2,1)} %param.22), kind=kOutput, calls=%fused_computation.24 | convolution fusion | flops 29360128 | bytes 1966080 | tf_op jit(solution)/shard_map/dot_general | solution.py:23
  71.3 2.8 %fusion.25 = f32[16,3584]{1,0:T(8,128)S(1)} fusion(bf16[1,1,3584,256]{3,2,1,0:T(8,128)(2,1)} %param.20, f32[16,256]{1,0:T(8,128)S(1)} %fusion.17, bf16[16,3584]{1,0:T(8,128)(2,1)S(1)} %squeeze.57, bf16[1,1,3584,256]{3,2,1,0:T(8,128)(2,1)S(1)} %copy-done, f32[16,256]{1,0:T(8,128)S(1)} %fusion.27), kind=kOutput, calls=%fused_computation.32 | convolution fusion | flops 58761216 | bytes 4046848 | tf_op jit(solution)/shard_map/dot_general | solution.py:23
  74.1 0.6 fusion.1
  74.8 0.8 pad_maximum_fusion.1
  75.6 4.1 %all-to-all-start.1 = ((bf16[2,4,4,3584]{3,2,0,1:T(4,128)(2,1)}), bf16[2,4,4,3584]{3,2,0,1:T(4,128)(2,1)S(1)}, u32[]{:S(2)}, u32[]{:S(2)}) async-start(bf16[2,4,4,3584]{3,2,0,1:T(4,128)(2,1)} %pad_maximum_fusion.1), calls=%async_computation.1 | async-start | bytes 458752 | tf_op jit(solution)/shard_map/all_to_all | solution.py:150
  79.7 3.0 %fusion.15 = f32[128,512]{1,0:T(8,128)S(1)} fusion(bf16[1,3584,512]{2,1,0:T(8,128)(2,1)} %param.23, bf16[256,3584]{1,0:T(8,128)(2,1)} %all-gather.3.cloned.1.call-done), kind=kOutput, calls=%fused_computation.22 | convolution fusion | flops 469762048 | bytes 4849664 | tf_op jit(solution)/shard_map/dot_general | solution.py:85
  82.7 2.4 %all-to-all-done.1 = bf16[2,4,4,3584]{3,2,0,1:T(4,128)(2,1)S(1)} async-done(((bf16[2,4,4,3584]{3,2,0,1:T(4,128)(2,1)}), bf16[2,4,4,3584]{3,2,0,1:T(4,128)(2,1)S(1)}, u32[]{:S(2)}, u32[]{:S(2)}) %all-to-all-start.1) | async-done | bytes 229408 | tf_op jit(solution)/shard_map/all_to_all | solution.py:150
  85.1 0.1 fusion.128
  85.3 1.7 %fusion.90 = f32[128,3584]{1,0:T(8,128)} fusion(bf16[16,3584]{1,0:T(8,128)(2,1)S(1)} %squeeze.58, bf16[16,128]{1,0:T(8,128)(2,1)S(1)} %bitcast.121, bf16[16,128]{1,0:T(8,128)(2,1)S(1)} %bitcast.120), kind=kOutput, calls=%fused_computation.73 | convolution fusion | flops 29835264 | bytes 1957888 | tf_op jit(solution)/shard_map/dot_general | solution.py:52
  86.9 6.4 %convolution_add_fusion.1 = f32[128,3584]{1,0:T(8,128)} fusion(f32[128,3584]{1,0:T(8,128)} %fusion.90, bf16[1,512,3584]{2,1,0:T(8,128)(2,1)} %param.25, bf16[1,3584,512]{2,1,0:T(8,128)(2,1)} %param.24, bf16[256,3584]{1,0:T(8,128)(2,1)} %all-gather.3.cloned.1.call-done, f32[128,512]{1,0:T(8,128)S(1)} %fusion.15), kind=kOutput, calls=%fused_computation.2 | convolution fusion | flops 940376064 | bytes 12189696 | tf_op jit(solution)/shard_map/dot_general | solution.py:88
  93.4 2.3 %constant_dynamic-slice_fusion = f32[128,1792]{1,0:T(8,128)} fusion(f32[128,3584]{1,0:T(8,128)} %convolution_add_fusion.1, s32[]{:T(128)S(6)} %select_n.74), kind=kLoop, calls=%fused_computation.125 | loop fusion | bytes 1835012 | tf_op jit(solution)/shard_map/dynamic_slice | solution.py:63
  95.7 0.0 collective-permute-start.2
  95.7 0.4 fusion.129
  96.1 2.8 %fusion = f32[128,3584]{1,0:T(8,128)S(1)} fusion(f32[128,3584]{1,0:T(8,128)S(1)} %fusion.129, f32[128,3584]{1,0:T(8,128)} %fusion.11, bf16[1,3584,512]{2,1,0:T(8,128)(2,1)S(1)} %copy-done.1, f32[128,512]{1,0:T(8,128)S(1)} %fusion.3, f32[128,512]{1,0:T(8,128)S(1)} %fusion.13), kind=kOutput, calls=%fused_computation.1 | convolution fusion | flops 471072768 | bytes 9699328 | tf_op jit(solution)/shard_map/dot_general | solution.py:23
  99.0 1.3 %copy-done.2 = f32[128,3584]{1,0:T(8,128)} copy-done((f32[128,3584]{1,0:T(8,128)}, f32[128,3584]{1,0:T(8,128)S(1)}, u32[]{:S(2)}) %copy-start.2) | copy-done | bytes 1835032
  100.2 1.0 constant_dynamic-slice_fusion.1
  101.2 0.5 collective-permute-start.3
  101.7 0.0 collective-permute-done.2
  101.8 2.2 %fusion.79 = bf16[1,128,1792]{2,1,0:T(8,128)(2,1)} fusion(f32[128,1792]{1,0:T(8,128)S(1)} %collective-permute-done.2, f32[128,3584]{1,0:T(8,128)} %convolution_add_fusion.1, s32[]{:T(128)S(6)} %select_n.72), kind=kLoop, calls=%fused_computation.59 | loop fusion | flops 458752 | bytes 2293764 | tf_op jit(solution)/shard_map/broadcast_in_dim | solution.py:173
  103.9 0.3 collective-permute-done.3
  104.2 2.0 %fusion.80 = bf16[1,128,1792]{2,1,0:T(8,128)(2,1)} fusion(f32[128,1792]{1,0:T(8,128)} %collective-permute-done.3, f32[128,3584]{1,0:T(8,128)S(1)} %copy-done.3, s32[]{:T(128)S(6)} %select_n.72), kind=kLoop, calls=%fused_computation.60 | loop fusion | flops 458752 | bytes 2293764 | tf_op jit(solution)/shard_map/broadcast_in_dim | solution.py:173
  (33 shorter events, 0.5 us)
Async XLA Ops:
  7.2 57.5 %copy-start = (bf16[1,1,3584,256]{3,2,1,0:T(8,128)(2,1)S(1)}, bf16[1,1,3584,256]{3,2,1,0:T(8,128)(2,1)}, u32[]{:S(2)}) copy-start(bf16[1,1,3584,256]{3,2,1,0:T(8,128)(2,1)} %param.21) | copy-start | bytes 5505028
  7.2 26.3 %copy-start.5 = (s32[2,1,128,8]{2,3,1,0:T(8,128)S(1)}, s32[2,1,128,8]{2,3,1,0:T(8,128)}, u32[]{:S(2)}) copy-start(s32[2,1,128,8]{2,3,1,0:T(8,128)} %param.19) | copy-start | bytes 24580
  7.2 26.3 %copy-start.6 = (s32[2,1,128,8]{2,3,1,0:T(8,128)S(1)}, s32[2,1,128,8]{2,3,1,0:T(8,128)}, u32[]{:S(2)}) copy-start(s32[2,1,128,8]{2,3,1,0:T(8,128)} %param.18) | copy-start | bytes 24580
  7.2 26.3 %copy-start.8 = (s32[2,1,128,8]{2,3,1,0:T(8,128)S(1)}, s32[2,1,128,8]{2,3,1,0:T(8,128)}, u32[]{:S(2)}) copy-start(s32[2,1,128,8]{2,3,1,0:T(8,128)} %param.17) | copy-start | bytes 24580
  7.2 26.3 %copy-start.7 = (s32[2,1,128,8]{2,3,1,0:T(8,128)S(1)}, s32[2,1,128,8]{2,3,1,0:T(8,128)}, u32[]{:S(2)}) copy-start(s32[2,1,128,8]{2,3,1,0:T(8,128)} %param.16) | copy-start | bytes 24580
  7.2 26.5 %copy-start.4 = (bf16[1,128,1792]{2,1,0:T(8,128)(2,1)S(1)}, bf16[1,128,1792]{2,1,0:T(8,128)(2,1)}, u32[]{:S(2)}) copy-start(bf16[1,128,1792]{2,1,0:T(8,128)(2,1)} %param.15) | copy-start | bytes 1376260
  7.2 36.5 %all-gather.3.cloned.1.call-start = ((), (), s32[]{:S(2)}) async-start(), calls=%async_computation.2 | async-start | bytes 2752512 | tf_op jit(solution)/shard_map/all_gather | solution.py:131
  7.3 16.8 %collective-permute-start = (bf16[128,1792]{1,0:T(8,128)(2,1)}, bf16[128,1792]{1,0:T(8,128)(2,1)S(1)}, u32[]{:S(2)}, u32[]{:S(2)}) collective-permute-start(bf16[128,1792]{1,0:T(8,128)(2,1)} %bitcast.124), channel_id=1, source_target_pairs={{24,0},{0,8},{8,16},{16,24},{25,1},{1,9},{9,17},{17,25},{26,2},{2,... | collective-permute-start | bytes 1376264 | tf_op jit(solution)/shard_map/ppermute | solution.py:10
  10.4 22.0 %collective-permute-start.1 = (bf16[128,1792]{1,0:T(8,128)(2,1)}, bf16[128,1792]{1,0:T(8,128)(2,1)S(1)}, u32[]{:S(2)}, u32[]{:S(2)}) collective-permute-start(bf16[128,1792]{1,0:T(8,128)(2,1)} %bitcast.125), channel_id=1, source_target_pairs={{8,0},{16,8},{24,16},{0,24},{9,1},{17,9},{25,17},{1,25},{10,2},{18... | collective-permute-start | bytes 1376264 | tf_op jit(solution)/shard_map/ppermute | solution.py:10
  47.6 14.0 %all-to-all-start = ((bf16[3,4,4,3584]{3,2,0,1:T(4,128)(2,1)}), bf16[3,4,4,3584]{3,2,0,1:T(4,128)(2,1)}, u32[]{:S(2)}, u32[]{:S(2)}) async-start(bf16[3,4,4,3584]{3,2,0,1:T(4,128)(2,1)} %bitcast.11), calls=%async_computation | async-start | bytes 688128 | tf_op jit(solution)/shard_map/all_to_all | solution.py:147
  75.6 9.5 %all-to-all-start.1 = ((bf16[2,4,4,3584]{3,2,0,1:T(4,128)(2,1)}), bf16[2,4,4,3584]{3,2,0,1:T(4,128)(2,1)S(1)}, u32[]{:S(2)}, u32[]{:S(2)}) async-start(bf16[2,4,4,3584]{3,2,0,1:T(4,128)(2,1)} %pad_maximum_fusion.1), calls=%async_computation.1 | async-start | bytes 458752 | tf_op jit(solution)/shard_map/all_to_all | solution.py:150
  93.4 2.8 %copy-start.1 = (bf16[1,3584,512]{2,1,0:T(8,128)(2,1)S(1)}, bf16[1,3584,512]{2,1,0:T(8,128)(2,1)}, u32[]{:S(2)}) copy-start(bf16[1,3584,512]{2,1,0:T(8,128)(2,1)} %param.24) | copy-start | bytes 11010052
  95.7 6.1 %collective-permute-start.2 = (f32[128,1792]{1,0:T(8,128)}, f32[128,1792]{1,0:T(8,128)S(1)}, u32[]{:S(2)}, u32[]{:S(2)}) collective-permute-start(f32[128,1792]{1,0:T(8,128)} %constant_dynamic-slice_fusion), channel_id=1, source_target_pairs={{1,0},{0,1},{3,2},{2,3},{5,4},{4,5},{7,6},{6,7},{9,8},{8,9},{11,10... | collective-permute-start | bytes 2752520 | tf_op jit(solution)/shard_map/ppermute | solution.py:10
  99.0 1.3 %copy-start.2 = (f32[128,3584]{1,0:T(8,128)}, f32[128,3584]{1,0:T(8,128)S(1)}, u32[]{:S(2)}) copy-start(f32[128,3584]{1,0:T(8,128)S(1)} %fusion) | copy-start | bytes 5505028
  101.2 3.0 %collective-permute-start.3 = (f32[128,1792]{1,0:T(8,128)}, f32[128,1792]{1,0:T(8,128)}, u32[]{:S(2)}, u32[]{:S(2)}) collective-permute-start(f32[128,1792]{1,0:T(8,128)} %constant_dynamic-slice_fusion.1), channel_id=1, source_target_pairs={{1,0},{0,1},{3,2},{2,3},{5,4},{4,5},{7,6},{6,7},{9,8},{8,9},{11,10... | collective-permute-start | bytes 2752520 | tf_op jit(solution)/shard_map/ppermute | solution.py:10
  101.7 2.4 %copy-start.3 = (f32[128,3584]{1,0:T(8,128)S(1)}, f32[128,3584]{1,0:T(8,128)}, u32[]{:S(2)}) copy-start(f32[128,3584]{1,0:T(8,128)} %copy-done.2) | copy-start | bytes 5505028
Sparse Core Ops, SparseCore 0:
  33.5 10.1 all-gather.2
